TPU v7x, 16 devices: a 4x2x1 block of a 4x4x8 slice. The times are simulated.
16 devices in a mesh: tasks: 2 (over y, z), group: 8 (over x, core).
Axes of the slice: x: 4, y: 2, z: 1, core: 2. Of those that a mesh axis runs over, the one named last changes fastest.
The devices are a block of a 4x4x8 slice.
Arguments:
- points: bfloat16 [32768, 384], P(('tasks', 'group')), parts along dimension 0
- vectors: bfloat16 [32768, 64], P(('tasks', 'group')), parts along dimension 0
- lengthscale: float32 [1], replicated
- outscale: float32 [1], replicated
Outputs:
- output: float32 [32768, 64], P(('tasks', 'group')), parts along dimension 0
There are 2 independent parts. A program takes and returns all parts, laid end to end along the dimension named above; an argument that names none is the same for every part.
All inputs are finite; a program needn't handle non-finite values.
Results may differ from a plain program's by a relative error of at most 0.001.
Values are sent between devices in bfloat16 or wider.
A program may use at most 768 MiB of HBM per device.

v0:
```python
import jax
import jax.numpy as jnp
from jax import lax
from jax.sharding import PartitionSpec as P


def row_norms(x_rows):
    return jnp.sum(jnp.square(x_rows.astype(jnp.float32)), axis=1)


def kernel_block(x_rows, norm_rows, x_cols, norm_cols, two_ell_sq, out_scale):
    gram_mat = jnp.einsum('nd,md->nm', x_rows, x_cols, preferred_element_type=jnp.float32)
    sq_dist = jnp.maximum(norm_rows[:, None] + norm_cols[None, :] - 2.0 * gram_mat, 0.0)
    return (out_scale * jnp.exp(-sq_dist / two_ell_sq)).astype(jnp.bfloat16)


def solution(mesh):
    n_group = mesh.shape['group']
    half_way = n_group // 2
    shift_left = [(source_idx, (source_idx - 1) % n_group) for source_idx in range(n_group)]
    send_back = [(source_idx, (source_idx + half_way - 1) % n_group) for source_idx in range(n_group)]
    row_spec = P(('tasks', 'group'), None)

    def local_fn(x_loc, v_loc, lengthscale, outscale):
        two_ell_sq = 2.0 * jnp.square(lengthscale[0])
        out_scale = outscale[0]
        norm_loc = row_norms(x_loc)

        def pair_step(x_vis, v_vis, y_acc, partner_acc):
            kern_pair = kernel_block(x_loc, norm_loc, x_vis, row_norms(x_vis), two_ell_sq, out_scale)
            y_acc = y_acc + jnp.dot(kern_pair, v_vis, preferred_element_type=jnp.float32)
            partner_acc = partner_acc + jnp.einsum('nm,nr->mr', kern_pair, v_loc, preferred_element_type=jnp.float32)
            return y_acc, partner_acc

        def loop_body(step_idx, carry):
            x_vis, v_vis, y_acc, partner_acc = carry
            x_vis = lax.ppermute(x_vis, 'group', shift_left)
            v_vis = lax.ppermute(v_vis, 'group', shift_left)
            partner_acc = lax.ppermute(partner_acc, 'group', shift_left)
            y_acc, partner_acc = pair_step(x_vis, v_vis, y_acc, partner_acc)
            return x_vis, v_vis, y_acc, partner_acc

        kern_diag = kernel_block(x_loc, norm_loc, x_loc, norm_loc, two_ell_sq, out_scale)
        y_acc = jnp.dot(kern_diag, v_loc, preferred_element_type=jnp.float32)
        x_vis = lax.ppermute(x_loc, 'group', shift_left)
        v_vis = lax.ppermute(v_loc, 'group', shift_left)
        y_acc, partner_acc = pair_step(x_vis, v_vis, y_acc, jnp.zeros(y_acc.shape, jnp.float32))
        x_vis, v_vis, y_acc, partner_acc = lax.fori_loop(2, half_way, loop_body, (x_vis, v_vis, y_acc, partner_acc))
        y_acc = y_acc + lax.ppermute(partner_acc, 'group', send_back)
        x_vis = lax.ppermute(x_vis, 'group', shift_left)
        v_vis = lax.ppermute(v_vis, 'group', shift_left)
        kern_far = kernel_block(x_loc, norm_loc, x_vis, row_norms(x_vis), two_ell_sq, out_scale)
        return y_acc + jnp.dot(kern_far, v_vis, preferred_element_type=jnp.float32)

    return jax.shard_map(local_fn, mesh=mesh, in_specs=(row_spec, row_spec, P(None), P(None)), out_specs=row_spec, check_vma=False)
```

profile of v0, /device:TPU:112, one launch (start us, length us, event | category | flops | bytes accessed | tf_op | source)
XLA Modules:
  0.0 237.3 jit_solution(3848008839779994792)
XLA Ops:
  0.0 3.4 %collective-permute-start.3 = (bf16[2048,384]{1,0:T(8,128)(2,1)}, bf16[2048,384]{1,0:T(8,128)(2,1)S(1)}, u32[]{:S(2)}, u32[]{:S(2)}) collective-permute-start(bf16[2048,384]{1,0:T(8,128)(2,1)} %param.6), channel_id=1, source_target_pairs={{0,7},{1,0},{2,1},{3,2},{4,3},{5,4},{6,5},{7,6},{8,15},{9,8},{10,9... | collective-permute-start | bytes 4718600 | tf_op jit(solution)/shard_map/ppermute | solution.py:45
  3.4 1.2 copy.5
  4.6 0.7 collective-permute-start.4
  5.3 1.8 multiply_reduce_fusion.3
  7.1 12.3 %multiply_subtract_fusion = f32[2048,2048]{0,1:T(8,128)} fusion(bf16[2048,384]{1,0:T(8,128)(2,1)} %param.6, f32[2048]{0:T(1024)S(1)} %multiply_reduce_fusion.3), kind=kOutput, calls=%fused_computation.12 | convolution fusion | flops 3233808384 | bytes 18358272 | tf_op jit(solution)/shard_map/nd,md->nm/dot_general | solution.py:12
  19.3 0.0 copy-start
  19.3 17.6 %copy.6 = f32[2048,2048]{1,0:T(8,128)} copy(f32[2048,2048]{0,1:T(8,128)} %multiply_subtract_fusion) | data formatting | bytes 33554432 | tf_op jit(solution)/shard_map/sub | solution.py:13
  38.3 0.0 copy-done
  38.3 7.8 %fusion.11 = f32[2048,64]{0,1:T(8,128)S(1)} fusion(bf16[2048,64]{0,1:T(8,128)(2,1)S(1)} %copy-done, f32[2048,2048]{1,0:T(8,128)} %copy.6, f32[]{:T(128)} %bitcast.1, f32[]{:T(128)} %bitcast.50), kind=kOutput, calls=%fused_computation.21 | convolution fusion | flops 557842432 | bytes 17563656 | tf_op jit(solution)/shard_map/dot_general | solution.py:44
  46.1 0.0 collective-permute-done.3
  46.1 0.0 copy-start.4
  46.1 0.4 multiply_reduce_fusion.2
  46.5 0.8 copy-done.4
  47.3 6.9 %broadcast_add_fusion.1 = f32[2048,2048]{0,1:T(8,128)} fusion(f32[2048]{0:T(1024)S(1)} %multiply_reduce_fusion.2, f32[2048]{0:T(1024)S(1)} %multiply_reduce_fusion.3), kind=kLoop, calls=%fused_computation.16 | loop fusion | flops 4194304 | bytes 16793600 | tf_op jit(solution)/shard_map/add | solution.py:13
  54.2 0.0 copy-start.2
  54.2 17.7 %copy.8 = f32[2048,2048]{1,0:T(8,128)} copy(f32[2048,2048]{0,1:T(8,128)} %broadcast_add_fusion.1) | data formatting | bytes 33554432 | tf_op jit(solution)/shard_map/add | solution.py:13
  71.9 0.0 copy-done.2
  71.9 10.1 %multiply_convert_fusion.1 = bf16[2048,2048]{1,0:T(8,128)(2,1)S(1)} fusion(f32[2048,2048]{1,0:T(8,128)} %copy.8, bf16[2048,384]{1,0:T(8,128)(2,1)S(1)} %copy-done.2, bf16[2048,384]{1,0:T(8,128)(2,1)} %copy-done.4, f32[]{:T(128)} %bitcast.1, f32[]{:T(128)} %bitcast.52), kind=kOutput, calls=%fused_computation.10 | convolution fusion | flops 3250585600 | bytes 28311560 | tf_op jit(solution)/shard_map/nd,md->nm/dot_general | solution.py:12
  81.9 0.0 copy-start.1
  81.9 2.4 %fusion.15 = f32[2048,64]{0,1:T(8,128)} fusion(bf16[2048,64]{0,1:T(8,128)(2,1)S(1)} %copy-done, bf16[2048,2048]{1,0:T(8,128)(2,1)S(1)} %multiply_convert_fusion.1), kind=kOutput, calls=%fused_computation.30 | convolution fusion | flops 536870912 | bytes 9175040 | tf_op jit(solution)/shard_map/nm,nr->mr/dot_general | solution.py:32
  84.3 0.0 collective-permute-done.4
  84.3 3.7 %convolution_add_fusion.2 = f32[2048,64]{0,1:T(8,128)S(1)} fusion(f32[2048,64]{0,1:T(8,128)S(1)} %fusion.11, bf16[2048,2048]{1,0:T(8,128)(2,1)S(1)} %multiply_convert_fusion.1, bf16[2048,64]{1,0:T(8,128)(2,1)} %collective-permute-done.4), kind=kOutput, calls=%fused_computation.25 | convolution fusion | flops 537001984 | bytes 9699328 | tf_op jit(solution)/shard_map/dot_general | solution.py:31
  88.0 0.0 copy-done.1
  88.1 82.7 %while.16 = (s32[]{:T(128)}, bf16[2048,384]{1,0:T(8,128)(2,1)}, bf16[2048,64]{1,0:T(8,128)(2,1)}, f32[2048,64]{0,1:T(8,128)S(1)}, f32[2048,64]{0,1:T(8,128)}, /*...) while((s32[]{:T(128)}, bf16[2048,384]{1,0:T(8,128)(2,1)}, ...), condition=%wide.region_4.0_spmd, body=%wide.region_2.0_spmd.sunk | while | flops 4331141120 | bytes 45637868 | solution.py:48
  88.3 0.2 collective-permute-start
  88.5 0.6 collective-permute-start.1
  89.1 0.1 collective-permute-start.2
  89.2 22.9 %collective-permute-done.1 = bf16[2048,64]{1,0:T(8,128)(2,1)S(1)} collective-permute-done((bf16[2048,64]{1,0:T(8,128)(2,1)}, bf16[2048,64]{1,0:T(8,128)(2,1)S(1)}, u32[]{:S(2)}, u32[]{:S(2)}) %collective-permute-start.1) | collective-permute-done | bytes 262176 | tf_op jit(solution)/shard_map/while/body/eval_jaxpr/ppermute | solution.py:38
  112.1 0.8 copy.22
  112.9 0.0 collective-permute-done
  112.9 1.1 copy.21
  114.0 0.4 multiply_reduce_fusion.5
  114.4 8.6 %multiply_convert_fusion.5 = bf16[2048,2048]{1,0:T(8,128)(2,1)S(1)} fusion(bf16[2048,384]{1,0:T(8,128)(2,1)} %get-tuple-element.174, bf16[2048,384]{1,0:T(8,128)(2,1)S(1)} %collective-permute-done, f32[]{:T(128)} %get-tuple-element.175, f32[2048]{0:T(1024)S(1)} %multiply_reduce_fusion.5, f32[2048]{0:T(1024)S(1)} %get-tuple-element.173, ...), kind=kOutput, calls=%fused_computation.clone.1 | convolution fusion | flops 3254779904 | bytes 11550728 | tf_op jit(solution)/shard_map/while/body/eval_jaxpr/nd,md->nm/dot_general | solution.py:12
  123.0 2.7 %convolution_add_fusion.5 = f32[2048,64]{0,1:T(8,128)S(1)} fusion(f32[2048,64]{0,1:T(8,128)S(1)} %get-tuple-element.159, bf16[2048,2048]{1,0:T(8,128)(2,1)S(1)} %multiply_convert_fusion.5, bf16[2048,64]{1,0:T(8,128)(2,1)S(1)} %collective-permute-done.1), kind=kOutput, calls=%fused_computation.3.clone.1 | convolution fusion | flops 537001984 | bytes 9699328 | tf_op jit(solution)/shard_map/while/body/eval_jaxpr/dot_general | solution.py:31
  125.7 0.0 collective-permute-done.2
  125.7 2.4 %convolution_add_fusion.6 = f32[2048,64]{0,1:T(8,128)} fusion(f32[2048,64]{0,1:T(8,128)S(1)} %collective-permute-done.2, bf16[2048,64]{0,1:T(8,128)(2,1)S(1)} %get-tuple-element.176, bf16[2048,2048]{1,0:T(8,128)(2,1)S(1)} %multiply_convert_fusion.5), kind=kOutput, calls=%fused_computation.2.clone.1 | convolution fusion | flops 537001984 | bytes 9699328 | tf_op jit(solution)/shard_map/while/body/eval_jaxpr/nm,nr->mr/dot_general | solution.py:32
  128.1 3.1 %collective-permute-start = (bf16[2048,384]{1,0:T(8,128)(2,1)}, bf16[2048,384]{1,0:T(8,128)(2,1)S(1)}, u32[]{:S(2)}, u32[]{:S(2)}) collective-permute-start(bf16[2048,384]{1,0:T(8,128)(2,1)} %get-tuple-element.157), channel_id=1, source_target_pairs={{0,7},{1,0},{2,1},{3,2},{4,3},{5,4},{6,5},{7,6},{8,15},{9,8},{10,9... | collective-permute-start | bytes 4718600 | tf_op jit(solution)/shard_map/while/body/eval_jaxpr/ppermute | solution.py:37
  131.2 0.0 collective-permute-start.1
  131.2 0.0 collective-permute-start.2
  131.3 23.5 %collective-permute-done.1 = bf16[2048,64]{1,0:T(8,128)(2,1)S(1)} collective-permute-done((bf16[2048,64]{1,0:T(8,128)(2,1)}, bf16[2048,64]{1,0:T(8,128)(2,1)S(1)}, u32[]{:S(2)}, u32[]{:S(2)}) %collective-permute-start.1) | collective-permute-done | bytes 262176 | tf_op jit(solution)/shard_map/while/body/eval_jaxpr/ppermute | solution.py:38
  154.7 0.8 copy.22
  155.5 0.0 collective-permute-done
  155.5 1.1 copy.21
  156.7 0.4 multiply_reduce_fusion.5
  157.1 8.6 %multiply_convert_fusion.5 = bf16[2048,2048]{1,0:T(8,128)(2,1)S(1)} fusion(bf16[2048,384]{1,0:T(8,128)(2,1)} %get-tuple-element.174, bf16[2048,384]{1,0:T(8,128)(2,1)S(1)} %collective-permute-done, f32[]{:T(128)} %get-tuple-element.175, f32[2048]{0:T(1024)S(1)} %multiply_reduce_fusion.5, f32[2048]{0:T(1024)S(1)} %get-tuple-element.173, ...), kind=kOutput, calls=%fused_computation.clone.1 | convolution fusion | flops 3254779904 | bytes 11550728 | tf_op jit(solution)/shard_map/while/body/eval_jaxpr/nd,md->nm/dot_general | solution.py:12
  165.6 2.7 %convolution_add_fusion.5 = f32[2048,64]{0,1:T(8,128)S(1)} fusion(f32[2048,64]{0,1:T(8,128)S(1)} %get-tuple-element.159, bf16[2048,2048]{1,0:T(8,128)(2,1)S(1)} %multiply_convert_fusion.5, bf16[2048,64]{1,0:T(8,128)(2,1)S(1)} %collective-permute-done.1), kind=kOutput, calls=%fused_computation.3.clone.1 | convolution fusion | flops 537001984 | bytes 9699328 | tf_op jit(solution)/shard_map/while/body/eval_jaxpr/dot_general | solution.py:31
  168.3 0.0 collective-permute-done.2
  168.3 2.4 %convolution_add_fusion.6 = f32[2048,64]{0,1:T(8,128)} fusion(f32[2048,64]{0,1:T(8,128)S(1)} %collective-permute-done.2, bf16[2048,64]{0,1:T(8,128)(2,1)S(1)} %get-tuple-element.176, bf16[2048,2048]{1,0:T(8,128)(2,1)S(1)} %multiply_convert_fusion.5), kind=kOutput, calls=%fused_computation.2.clone.1 | convolution fusion | flops 537001984 | bytes 9699328 | tf_op jit(solution)/shard_map/while/body/eval_jaxpr/nm,nr->mr/dot_general | solution.py:32
  170.8 3.1 %collective-permute-start.6 = (bf16[2048,384]{1,0:T(8,128)(2,1)}, bf16[2048,384]{1,0:T(8,128)(2,1)S(1)}, u32[]{:S(2)}, u32[]{:S(2)}) collective-permute-start(bf16[2048,384]{1,0:T(8,128)(2,1)} %get-tuple-element.62), channel_id=1, source_target_pairs={{0,7},{1,0},{2,1},{3,2},{4,3},{5,4},{6,5},{7,6},{8,15},{9,8},{10,9... | collective-permute-start | bytes 4718600 | tf_op jit(solution)/shard_map/ppermute | solution.py:50
  173.9 0.0 collective-permute-start.5
  173.9 1.3 collective-permute-start.7
  175.2 20.9 %collective-permute-done.6 = bf16[2048,384]{1,0:T(8,128)(2,1)S(1)} collective-permute-done((bf16[2048,384]{1,0:T(8,128)(2,1)}, bf16[2048,384]{1,0:T(8,128)(2,1)S(1)}, u32[]{:S(2)}, u32[]{:S(2)}) %collective-permute-start.6) | collective-permute-done | bytes 1572896 | tf_op jit(solution)/shard_map/ppermute | solution.py:50
  196.1 0.0 copy-start.5
  196.1 1.1 copy-done.5
  197.2 0.4 multiply_reduce_fusion.1
  197.6 6.9 %broadcast_add_fusion = f32[2048,2048]{0,1:T(8,128)} fusion(f32[2048]{0:T(1024)S(1)} %multiply_reduce_fusion.1, f32[2048]{0:T(1024)S(1)} %get-tuple-element.190), kind=kLoop, calls=%fused_computation.15 | loop fusion | flops 4194304 | bytes 16793600 | tf_op jit(solution)/shard_map/add | solution.py:13
  204.5 0.0 copy-start.3
  204.5 17.7 %copy.9 = f32[2048,2048]{1,0:T(8,128)} copy(f32[2048,2048]{0,1:T(8,128)} %broadcast_add_fusion) | data formatting | bytes 33554432 | tf_op jit(solution)/shard_map/add | solution.py:13
  222.2 0.0 collective-permute-done.7
  222.2 0.0 collective-permute-done.5
  222.2 0.0 copy-done.3
  222.2 15.1 %add_add_fusion = f32[2048,64]{0,1:T(8,128)} fusion(f32[2048,64]{0,1:T(8,128)S(1)} %get-tuple-element.60, f32[2048,64]{0,1:T(8,128)S(1)} %collective-permute-done.5, bf16[2048,64]{1,0:T(8,128)(2,1)S(1)} %collective-permute-done.7, f32[2048,2048]{1,0:T(8,128)} %copy.9, bf16[2048,384]{1,0:T(8,128)(2,1)} %copy-done.5, bf16[2048,384]{1,0:T(8,128)(2,1)S(1)} %copy-done.3, ...), kind=kOutput, calls=%fused_computation.26 | convolution fusion | flops 3787718656 | bytes 21757960 | tf_op jit(solution)/shard_map/dot_general | solution.py:53
Async XLA Ops:
  0.0 46.1 %collective-permute-start.3 = (bf16[2048,384]{1,0:T(8,128)(2,1)}, bf16[2048,384]{1,0:T(8,128)(2,1)S(1)}, u32[]{:S(2)}, u32[]{:S(2)}) collective-permute-start(bf16[2048,384]{1,0:T(8,128)(2,1)} %param.6), channel_id=1, source_target_pairs={{0,7},{1,0},{2,1},{3,2},{4,3},{5,4},{6,5},{7,6},{8,15},{9,8},{10,9... | collective-permute-start | bytes 4718600 | tf_op jit(solution)/shard_map/ppermute | solution.py:45
  4.6 79.7 %collective-permute-start.4 = (bf16[2048,64]{1,0:T(8,128)(2,1)S(1)}, bf16[2048,64]{1,0:T(8,128)(2,1)}, u32[]{:S(2)}, u32[]{:S(2)}) collective-permute-start(bf16[2048,64]{1,0:T(8,128)(2,1)S(1)} %copy.5), channel_id=1, source_target_pairs={{0,7},{1,0},{2,1},{3,2},{4,3},{5,4},{6,5},{7,6},{8,15},{9,8},{10,9... | collective-permute-start | bytes 786440 | tf_op jit(solution)/shard_map/ppermute | solution.py:46
  19.3 18.9 %copy-start = (bf16[2048,64]{0,1:T(8,128)(2,1)S(1)}, bf16[2048,64]{0,1:T(8,128)(2,1)}, u32[]{:S(2)}) copy-start(bf16[2048,64]{0,1:T(8,128)(2,1)} %param.7) | copy-start | bytes 786436
  46.1 1.1 copy-start.4
  54.2 17.7 %copy-start.2 = (bf16[2048,384]{1,0:T(8,128)(2,1)S(1)}, bf16[2048,384]{1,0:T(8,128)(2,1)}, u32[]{:S(2)}) copy-start(bf16[2048,384]{1,0:T(8,128)(2,1)} %param.6) | copy-start | bytes 4718596
  81.9 6.1 %copy-start.1 = (bf16[2048,64]{0,1:T(8,128)(2,1)S(1)}, bf16[2048,64]{0,1:T(8,128)(2,1)}, u32[]{:S(2)}) copy-start(bf16[2048,64]{0,1:T(8,128)(2,1)} %param.7) | copy-start | bytes 786436
  88.3 24.6 %collective-permute-start = (bf16[2048,384]{1,0:T(8,128)(2,1)}, bf16[2048,384]{1,0:T(8,128)(2,1)S(1)}, u32[]{:S(2)}, u32[]{:S(2)}) collective-permute-start(bf16[2048,384]{1,0:T(8,128)(2,1)} %get-tuple-element.157), channel_id=1, source_target_pairs={{0,7},{1,0},{2,1},{3,2},{4,3},{5,4},{6,5},{7,6},{8,15},{9,8},{10,9... | collective-permute-start | bytes 4718600 | tf_op jit(solution)/shard_map/while/body/eval_jaxpr/ppermute | solution.py:37
  88.5 23.5 %collective-permute-start.1 = (bf16[2048,64]{1,0:T(8,128)(2,1)}, bf16[2048,64]{1,0:T(8,128)(2,1)S(1)}, u32[]{:S(2)}, u32[]{:S(2)}) collective-permute-start(bf16[2048,64]{1,0:T(8,128)(2,1)} %get-tuple-element.158), channel_id=1, source_target_pairs={{0,7},{1,0},{2,1},{3,2},{4,3},{5,4},{6,5},{7,6},{8,15},{9,8},{10,9... | collective-permute-start | bytes 786440 | tf_op jit(solution)/shard_map/while/body/eval_jaxpr/ppermute | solution.py:38
  89.1 36.5 %collective-permute-start.2 = (f32[2048,64]{0,1:T(8,128)}, f32[2048,64]{0,1:T(8,128)S(1)}, u32[]{:S(2)}, u32[]{:S(2)}) collective-permute-start(f32[2048,64]{0,1:T(8,128)} %get-tuple-element.160), channel_id=1, source_target_pairs={{0,7},{1,0},{2,1},{3,2},{4,3},{5,4},{6,5},{7,6},{8,15},{9,8},{10,9... | collective-permute-start | bytes 1572872 | tf_op jit(solution)/shard_map/while/body/eval_jaxpr/ppermute | solution.py:39
  128.1 27.5 %collective-permute-start = (bf16[2048,384]{1,0:T(8,128)(2,1)}, bf16[2048,384]{1,0:T(8,128)(2,1)S(1)}, u32[]{:S(2)}, u32[]{:S(2)}) collective-permute-start(bf16[2048,384]{1,0:T(8,128)(2,1)} %get-tuple-element.157), channel_id=1, source_target_pairs={{0,7},{1,0},{2,1},{3,2},{4,3},{5,4},{6,5},{7,6},{8,15},{9,8},{10,9... | collective-permute-start | bytes 4718600 | tf_op jit(solution)/shard_map/while/body/eval_jaxpr/ppermute | solution.py:37
  131.2 23.5 %collective-permute-start.1 = (bf16[2048,64]{1,0:T(8,128)(2,1)}, bf16[2048,64]{1,0:T(8,128)(2,1)S(1)}, u32[]{:S(2)}, u32[]{:S(2)}) collective-permute-start(bf16[2048,64]{1,0:T(8,128)(2,1)} %get-tuple-element.158), channel_id=1, source_target_pairs={{0,7},{1,0},{2,1},{3,2},{4,3},{5,4},{6,5},{7,6},{8,15},{9,8},{10,9... | collective-permute-start | bytes 786440 | tf_op jit(solution)/shard_map/while/body/eval_jaxpr/ppermute | solution.py:38
  131.2 37.1 %collective-permute-start.2 = (f32[2048,64]{0,1:T(8,128)}, f32[2048,64]{0,1:T(8,128)S(1)}, u32[]{:S(2)}, u32[]{:S(2)}) collective-permute-start(f32[2048,64]{0,1:T(8,128)} %get-tuple-element.160), channel_id=1, source_target_pairs={{0,7},{1,0},{2,1},{3,2},{4,3},{5,4},{6,5},{7,6},{8,15},{9,8},{10,9... | collective-permute-start | bytes 1572872 | tf_op jit(solution)/shard_map/while/body/eval_jaxpr/ppermute | solution.py:39
  170.8 25.3 %collective-permute-start.6 = (bf16[2048,384]{1,0:T(8,128)(2,1)}, bf16[2048,384]{1,0:T(8,128)(2,1)S(1)}, u32[]{:S(2)}, u32[]{:S(2)}) collective-permute-start(bf16[2048,384]{1,0:T(8,128)(2,1)} %get-tuple-element.62), channel_id=1, source_target_pairs={{0,7},{1,0},{2,1},{3,2},{4,3},{5,4},{6,5},{7,6},{8,15},{9,8},{10,9... | collective-permute-start | bytes 4718600 | tf_op jit(solution)/shard_map/ppermute | solution.py:50
  173.9 48.3 %collective-permute-start.5 = (f32[2048,64]{0,1:T(8,128)}, f32[2048,64]{0,1:T(8,128)S(1)}, u32[]{:S(2)}, u32[]{:S(2)}) collective-permute-start(f32[2048,64]{0,1:T(8,128)} %get-tuple-element.61), channel_id=1, source_target_pairs={{0,3},{1,4},{2,5},{3,6},{4,7},{5,0},{6,1},{7,2},{8,11},{9,12},{10,... | collective-permute-start | bytes 1572872 | tf_op jit(solution)/shard_map/ppermute | solution.py:49
  173.9 48.3 %collective-permute-start.7 = (bf16[2048,64]{1,0:T(8,128)(2,1)}, bf16[2048,64]{1,0:T(8,128)(2,1)S(1)}, u32[]{:S(2)}, u32[]{:S(2)}) collective-permute-start(bf16[2048,64]{1,0:T(8,128)(2,1)} %get-tuple-element.63), channel_id=1, source_target_pairs={{0,7},{1,0},{2,1},{3,2},{4,3},{5,4},{6,5},{7,6},{8,15},{9,8},{10,9... | collective-permute-start | bytes 786440 | tf_op jit(solution)/shard_map/ppermute | solution.py:51
  196.1 1.1 copy-start.5
  204.5 17.7 %copy-start.3 = (bf16[2048,384]{1,0:T(8,128)(2,1)S(1)}, bf16[2048,384]{1,0:T(8,128)(2,1)}, u32[]{:S(2)}) copy-start(bf16[2048,384]{1,0:T(8,128)(2,1)} %get-tuple-element.182) | copy-start | bytes 4718596
where the time goes:
time: 238 us; the launch traced here: 237 us
  matrix products  78.7 us (33%)
  waiting for transfers between devices  67.2 us (28%)
  local copies, waits for them, and re-layouts  60.1 us (25%)
  other arithmetic  17 us (7%)
  starting transfers between devices  12.6 us (5%)
    ppermute x2, waiting for transfers between devices, loop_body(): v_vis = lax.ppermute(v_vis, 'group', shift_left)  46.3 us
    dot_general x4, matrix products, kernel_block(): jnp.einsum('nd,md->nm', x_rows, x_cols, preferred_element_type=jnp.float32)  39.4 us
    add x2, local copies, waits for them, and re-layouts, kernel_block(): norm_rows[:, None] + norm_cols[None, :] - 2.0 * gram_mat  35.4 us
    ppermute x1, waiting for transfers between devices, local_fn(): x_vis = lax.ppermute(x_vis, 'group', shift_left)  20.9 us
    sub x1, local copies, waits for them, and re-layouts, kernel_block(): norm_rows[:, None] + norm_cols[None, :] - 2.0 * gram_mat  17.6 us
    dot_general x1, matrix products, local_fn(): return y_acc + jnp.dot(kern_far, v_vis, preferred_element_type=jnp.float32)  15.1 us
    add x2, other arithmetic, kernel_block(): norm_rows[:, None] + norm_cols[None, :] - 2.0 * gram_mat  13.7 us
    dot_general x3, matrix products, pair_step(): jnp.dot(kern_pair, v_vis, preferred_element_type=jnp.float32)  9.09 us
  transfers between devices with their start and end apart: 11, of which 3 were waited for; matrix products, arithmetic and copies ran while one was open for 55% of the time, Pallas kernels for 0%

commit v1 on v0

v1 whole, which is shorter than its diff:
```python
import functools

import jax
import jax.numpy as jnp
from jax import lax
from jax.experimental import pallas as pl
from jax.experimental.pallas import tpu as pltpu
from jax.sharding import PartitionSpec as P

CH = 256
LOG2E = 1.4426950408889634
OWN, SIB, LFT, RGT, LFT2, RGT2 = 0, 8, 16, 24, 32, 40
N_STEPS = 32


def ext_values(x):
    xf = x.astype(jnp.float32)
    h = -0.5 * jnp.sum(xf * xf, axis=1, keepdims=True)
    hi = h.astype(jnp.bfloat16).astype(jnp.float32)
    r = jnp.where(h == hi, 0.0, h - hi)
    mid = r.astype(jnp.bfloat16).astype(jnp.float32)
    return hi, mid, r - mid


def ext_rows(x, first):
    hi, mid, lo = ext_values(x)
    lane = lax.broadcasted_iota(jnp.int32, (x.shape[0], 128), 1)
    e = jnp.where(lane < 6, 1.0, 0.0)
    e = jnp.where(lane == first, hi, e)
    e = jnp.where(lane == first + 1, mid, e)
    e = jnp.where(lane == first + 2, lo, e)
    return e.astype(jnp.bfloat16)


def describe(t):
    w = jnp.where
    early = t < 8
    mid = (t >= 8) & (t < 16)
    u = jnp.maximum(t - 19, 0)
    is_new_far = (t >= 19) & (t <= 28) & (lax.rem(u, 3) == 0)
    m = t - 16 - w(t >= 20, jnp.minimum((jnp.maximum(t - 20, 0)) // 3 + 1, 4), 0)
    is_far = (t >= 16) & (is_new_far | (m < 4))
    q = w(mid, (t - 8) // 2, w(is_new_far, 4 + u // 3, w(m < 4, m, 4 + (m - 4) // 2)))
    second = w(mid, lax.rem(t, 2), lax.rem(jnp.maximum(m, 0), 2)) == 1
    q = w(early, 0, q)
    own_a = w(early, 2 * t, w(second, LFT2, LFT) + q)
    own_b = w(early, 2 * t + 1, w(second, RGT2, RGT) + q)
    a0 = w(is_far, LFT + q, own_a)
    b0 = w(is_far, LFT2 + q, own_b)
    a1 = w(is_far, RGT + q, own_a)
    b1 = w(is_far, RGT2 + q, own_b)
    return a0, b0, a1, b1, w(is_far, 8, 0)


def kernel(n, x_hbm, vt_hbm, sc_ref, out_ref,
           xb, vb, xe, xr, ka, kb, y, part, pin,
           loc_sem, sx, sv, rx, rv, ps, pr):
    me = lax.axis_index("group")
    core = lax.rem(me, 2)
    sib = me + 1 - 2 * core
    left = lax.rem(me + n - 2, n)
    right = lax.rem(me + 2, n)

    def remote(src, dst, ssem, rsem, dev):
        return pltpu.make_async_remote_copy(
            src_ref=src, dst_ref=dst, send_sem=ssem, recv_sem=rsem,
            device_id={"group": dev}, device_id_type=pl.DeviceIdType.MESH)

    own_x = pltpu.make_async_copy(x_hbm, xb.at[pl.ds(OWN, 8)], loc_sem.at[0])
    own_v = pltpu.make_async_copy(vt_hbm, vb.at[pl.ds(OWN, 8)], loc_sem.at[1])
    own_x.start()
    own_v.start()
    barrier = pltpu.get_barrier_semaphore()
    for dev in (sib, left, right):
        pl.semaphore_signal(barrier, inc=1, device_id={"group": dev},
                            device_id_type=pl.DeviceIdType.MESH)
    own_x.wait()
    own_v.wait()
    pl.semaphore_wait(barrier, 3)

    def to_left(q, o):
        return (remote(xb.at[OWN + o], xb.at[LFT + q], sx.at[q], rx.at[LFT + q], left),
                remote(vb.at[OWN + o], vb.at[LFT + q], sv.at[q], rv.at[LFT + q], left))

    def to_right(q, o):
        return (remote(xb.at[OWN + o], xb.at[RGT + q], sx.at[8 + q], rx.at[RGT + q], right),
                remote(vb.at[OWN + o], vb.at[RGT + q], sv.at[8 + q], rv.at[RGT + q], right))

    def to_sib():
        return (remote(xb.at[pl.ds(OWN, 8)], xb.at[pl.ds(SIB, 8)], sx.at[16], rx.at[SIB], sib),
                remote(vb.at[pl.ds(OWN, 8)], vb.at[pl.ds(SIB, 8)], sv.at[16], rv.at[SIB], sib))

    def fwd(q):
        return (remote(xb.at[LFT + q], xb.at[LFT2 + q], sx.at[17 + q], rx.at[LFT2 + q], sib),
                remote(vb.at[LFT + q], vb.at[LFT2 + q], sv.at[17 + q], rv.at[LFT2 + q], sib),
                remote(xb.at[RGT + q], xb.at[RGT2 + q], sx.at[25 + q], rx.at[RGT2 + q], sib),
                remote(vb.at[RGT + q], vb.at[RGT2 + q], sv.at[25 + q], rv.at[RGT2 + q], sib))

    def partial_copies():
        return (remote(part.at[pl.ds(0, 4)], pin.at[pl.ds(0, 4)], ps.at[0], pr.at[0], left),
                remote(part.at[pl.ds(4, 4)], pin.at[pl.ds(4, 4)], ps.at[1], pr.at[1], right))

    for q in range(8):
        for c in to_left(q, (q + 4) % 8) + to_right(q, q):
            c.start()
        if q == 0:
            for c in to_sib():
                c.start()

    two_ell_sq = 2.0 * sc_ref[0] * sc_ref[0]

    def target(slot, tile):
        xv = xb[slot]
        full = jnp.concatenate([xv, ext_rows(xv, 3)], axis=1)
        xr[tile] = full.T

    lax.fori_loop(0, 8, lambda i, _: (target(OWN + i, i), 0)[1], 0)
    y[...] = jnp.zeros_like(y)
    kb[...] = jnp.zeros_like(kb)

    c2 = sc_ref[2]
    ls = sc_ref[3]

    def gram(d, dst):
        a0, b0, a1, b1, tb = d
        for g, (a, b) in enumerate(((a0, b0), (a1, b1))):
            lhs = jnp.concatenate(
                [jnp.concatenate([xb[a], xe[a]], axis=1),
                 jnp.concatenate([xb[b], xe[b]], axis=1)], axis=0)
            for i in range(4):
                s = jnp.dot(lhs, xr[tb + 4 * g + i], preferred_element_type=jnp.float32)
                e = jnp.minimum(s, 0.0) * c2 + ls
                dst[4 * g + i] = jnp.exp2(e).astype(jnp.bfloat16)
                yield

    def kv(d, src):
        a0, b0, a1, b1, tb = d
        for g, (a, b) in enumerate(((a0, b0), (a1, b1))):
            lhs = jnp.concatenate([vb[a], vb[b]], axis=1)
            for i in range(4):
                y[tb + 4 * g + i] += jnp.dot(lhs, src[4 * g + i], preferred_element_type=jnp.float32)
                yield

    def run(cur, prev, dst, src):
        gs, ks = gram(cur, dst), kv(prev, src)
        for i in range(8):
            next(gs)
            next(ks)

    def arrive(q):
        for s in (LFT + q, RGT + q):
            remote(xb.at[s], xb.at[s], sx.at[0], rx.at[s], sib).wait_recv()
            remote(vb.at[s], vb.at[s], sv.at[0], rv.at[s], sib).wait_recv()
        for c in fwd(q):
            c.start()

    def arrive2(q):
        for s in (LFT2 + q, RGT2 + q):
            remote(xb.at[s], xb.at[s], sx.at[0], rx.at[s], sib).wait_recv()
            remote(vb.at[s], vb.at[s], sv.at[0], rv.at[s], sib).wait_recv()

    def step(t, dst, src):
        d = describe(t)
        p = describe(jnp.maximum(t - 1, 0))

        @pl.when(t == 4)
        def _():
            for c in to_sib():
                c.wait_recv()

        mid = (t >= 8) & (t < 16)
        late = jnp.maximum(t - 18, 0)
        is_late = (t >= 18) & (t <= 28)
        first = (mid & (lax.rem(t, 2) == 0)) | (is_late & (lax.rem(late, 3) == 0))
        secnd = (mid & (lax.rem(t, 2) == 1)) | (is_late & (lax.rem(late, 3) == 1))
        q = jnp.where(mid, (t - 8) // 2, 4 + late // 3)
        q = jnp.minimum(jnp.maximum(q, 0), 7)

        @pl.when(first)
        def _():
            arrive(q)

        @pl.when(secnd)
        def _():
            arrive2(q)

        pa = jnp.where(t < 8, 2 * t, jnp.where(first, LFT + q, jnp.where(secnd, LFT2 + q, 0)))
        pb = jnp.where(t < 8, 2 * t + 1, jnp.where(first, RGT + q, jnp.where(secnd, RGT2 + q, 1)))

        @pl.when(t == 16)
        def _():
            lax.fori_loop(0, 4, lambda i, _: (target(RGT + i, 8 + i), 0)[1], 0)
            lax.fori_loop(0, 4, lambda i, _: (target(LFT + i, 12 + i), 0)[1], 0)

        xe[pa] = ext_rows(xb[pa], 0)
        xe[pb] = ext_rows(xb[pb], 0)
        run(d, p, dst, src)

        @pl.when(t == 29)
        def _():
            for i in range(8):
                part[i] = y[8 + i]
            for c in partial_copies():
                c.start()

    def body(u, _):
        step(2 * u, ka, kb)
        step(2 * u + 1, kb, ka)
        return 0

    lax.fori_loop(0, N_STEPS // 2, body, 0)
    for _ in kv(describe(jnp.int32(N_STEPS - 1)), kb):
        pass

    for c in partial_copies():
        c.wait()
    for i in range(8):
        out_ref[:, i * CH:(i + 1) * CH] = y[i] + pin[i]

    for q in range(8):
        for c in to_left(q, (q + 4) % 8) + to_right(q, q) + fwd(q):
            c.wait_send()
    for c in to_sib():
        c.wait_send()


def solution(mesh):
    n = mesh.shape["group"]
    row_spec = P(("tasks", "group"), None)

    def local_fn(x_loc, v_loc, lengthscale, outscale):
        rows, feat = x_loc.shape
        rhs = v_loc.shape[1]
        nc = rows // CH
        x3 = x_loc.reshape(nc, CH, feat)
        vt = v_loc.reshape(nc, CH, rhs).transpose(0, 2, 1)
        two_ell_sq = 2.0 * jnp.square(lengthscale[0])
        sc = jnp.stack([two_ell_sq, outscale[0], 2.0 * LOG2E / two_ell_sq, jnp.log2(outscale[0])])
        bf = jnp.bfloat16
        dma = pltpu.SemaphoreType.DMA
        yt = pl.pallas_call(
            functools.partial(kernel, n),
            out_shape=jax.ShapeDtypeStruct((rhs, rows), jnp.float32),
            in_specs=[pl.BlockSpec(memory_space=pl.ANY), pl.BlockSpec(memory_space=pl.ANY),
                      pl.BlockSpec(memory_space=pltpu.SMEM)],
            out_specs=pl.BlockSpec(memory_space=pltpu.VMEM),
            scratch_shapes=[
                pltpu.VMEM((6 * nc, CH, feat), bf),
                pltpu.VMEM((6 * nc, rhs, CH), bf),
                pltpu.VMEM((6 * nc, CH, 128), bf),
                pltpu.VMEM((2 * nc, feat + 128, CH), bf),
                pltpu.VMEM((nc, 2 * CH, CH), bf),
                pltpu.VMEM((nc, 2 * CH, CH), bf),
                pltpu.VMEM((2 * nc, rhs, CH), jnp.float32),
                pltpu.VMEM((nc, rhs, CH), jnp.float32),
                pltpu.VMEM((nc, rhs, CH), jnp.float32),
                dma((2,)), dma((40,)), dma((40,)), dma((6 * nc,)), dma((6 * nc,)), dma((2,)), dma((2,)),
            ],
            compiler_params=pltpu.CompilerParams(
                collective_id=0, has_side_effects=True, vmem_limit_bytes=56 * 2**20),
        )(x3, vt, sc)
        return yt.T

    return jax.shard_map(local_fn, mesh=mesh, in_specs=(row_spec, row_spec, P(None), P(None)),
                         out_specs=row_spec, check_vma=False)
```

time: 238 us -> 76 us (0.32)
  matrix products: 78.7 us -> 0 us
  Pallas kernels: 0 us -> 70.2 us
  waiting for transfers between devices: 67.2 us -> 0 us
  local copies, waits for them, and re-layouts: 60.1 us -> 3.54 us
  other arithmetic: 17 us -> 0.67 us
  starting transfers between devices: 12.6 us -> 0 us
    dot_general x12 -> x0, matrix products: 78.7 us -> none  [the longest x4 39.4 us: kernel_block(): jnp.einsum('nd,md->nm', x_rows, x_cols, preferred_element_type=jnp.float32)]
    pallas_call x0 -> x1, Pallas kernels: none -> 70.2 us  [local_fn(): pl.pallas_call(functools.partial(kernel, n), out_shape=jax.ShapeDtypeStru...]
    ppermute x11 -> x0, waiting for transfers between devices: 67.2 us -> none  [the longest x2 46.3 us: loop_body(): v_vis = lax.ppermute(v_vis, 'group', shift_left)]
    add x2 -> x0, local copies, waits for them, and re-layouts: 35.4 us -> none  [kernel_block(): norm_rows[:, None] + norm_cols[None, :] - 2.0 * gram_mat]
    sub x1 -> x0, local copies, waits for them, and re-layouts: 17.6 us -> none  [kernel_block(): norm_rows[:, None] + norm_cols[None, :] - 2.0 * gram_mat]
    add x2 -> x0, other arithmetic: 13.7 us -> none  [kernel_block(): norm_rows[:, None] + norm_cols[None, :] - 2.0 * gram_mat]
    ppermute x11 -> x0, starting transfers between devices: 12.6 us -> none  [the longest x1 3.39 us: local_fn(): x_vis = lax.ppermute(x_loc, 'group', shift_left)]
    while x4 -> x0, local copies, waits for them, and re-layouts: 3.88 us -> none
  transfers between devices with their start and end apart: 11 -> 0, of which waited for: 3 -> 0; matrix products, arithmetic and copies ran while one was open for 55% -> 0% of each run, Pallas kernels for 0% -> 0%
where the time goes in v1:
time: 76 us; the launch traced here: 75.8 us
  Pallas kernels  70.2 us (92%)
  local copies, waits for them, and re-layouts  3.54 us (5%)
  between operations  1.39 us (2%)
    pallas_call x1, Pallas kernels, local_fn(): pl.pallas_call(functools.partial(kernel, n), out_shape=jax.ShapeDtypeStru...  70.2 us
    unnamed x1, local copies, waits for them, and re-layouts  1.87 us
    reshape x1, local copies, waits for them, and re-layouts, local_fn(): vt = v_loc.reshape(nc, CH, rhs).transpose(0, 2, 1)  1.67 us

profile of v1, /device:TPU:112, one launch (start us, length us, event | category | flops | bytes accessed | tf_op | source)
XLA Modules:
  0.0 75.8 jit_solution(14328117242687766574)
XLA Ops:
  1.4 0.7 pad_maximum_fusion.sc_ref
  2.1 1.7 %copy.8 = bf16[8,8,8,256]{3,2,0,1:T(8,128)(2,1)} copy(bf16[8,8,8,256]{3,2,1,0:T(8,128)(2,1)} %bitcast.12) | data formatting | bytes 524288 | tf_op jit(solution)/shard_map/reshape | solution.py:236
  3.7 70.2 %shard_map.46 = f32[64,2048]{1,0:T(8,128)} custom-call(bf16[8,256,384]{2,1,0:T(8,128)(2,1)} %bitcast.10, bf16[8,64,256]{2,1,0:T(8,128)(2,1)} %bitcast.11, f32[4]{0:T(128)} %pad_maximum_fusion.sc_ref), custom_call_target="tpu_custom_call" | custom-call | tf_op jit(solution)/shard_map/pallas_call | solution.py:241
  74.0 1.9 %copy.12 = f32[2048,64]{0,1:T(8,128)} copy(f32[2048,64]{0,1:T(8,128)} %bitcast.9) | data formatting | bytes 1048576

commit v2 on v1

v2 whole, which is shorter than its diff:
```python
import functools

import jax
import jax.numpy as jnp
from jax import lax
from jax.experimental import pallas as pl
from jax.experimental.pallas import tpu as pltpu
from jax.sharding import PartitionSpec as P

CH = 256
LOG2E = 1.4426950408889634
OWN, SIB, LFT, RGT, LFT2, RGT2 = 0, 8, 16, 24, 32, 40
MAIN_BLOCKS = 14
LATE_STEPS = (("F", 0), ("F", 1), ("F", 2), ("F", 3), ("F", 4), ("A", 4),
              ("F", 5), ("B", 4), ("A", 5), ("B", 5), ("F", 6), ("A", 6))


def ext_values(x):
    xf = x.astype(jnp.float32)
    h = -0.5 * jnp.sum(xf * xf, axis=1, keepdims=True)
    hi = h.astype(jnp.bfloat16).astype(jnp.float32)
    r = jnp.where(h == hi, 0.0, h - hi)
    mid = r.astype(jnp.bfloat16).astype(jnp.float32)
    return hi, mid, r - mid


def ext_rows(x, *firsts):
    hi, mid, lo = ext_values(x)
    lane = lax.broadcasted_iota(jnp.int32, (x.shape[0], 128), 1)
    ones = jnp.where(lane < 6, 1.0, 0.0)
    out = []
    for first in firsts:
        e = jnp.where(lane == first, hi, ones)
        e = jnp.where(lane == first + 1, mid, e)
        e = jnp.where(lane == first + 2, lo, e)
        out.append(e.astype(jnp.bfloat16))
    return out


PREP = [(0, 1, 0, 1), (0, 1, 0, 1), (8, 9, 10, 11), (12, 13, 14, 15)]
PREP += [(LFT + q, RGT + q, LFT2 + q, RGT2 + q) for q in range(4)]
PREP += [(0, 1, 0, 1), (0, 1, LFT + 4, RGT + 4), (LFT2 + 4, RGT2 + 4, LFT + 5, RGT + 5),
         (LFT2 + 5, RGT2 + 5, 0, 1), (0, 1, LFT + 6, RGT + 6), (LFT2 + 6, RGT2 + 6, 0, 1)]


def pick(t, first, values):
    out = jnp.int32(values[0])
    for k, v in enumerate(values[1:], 1):
        if v != values[k - 1]:
            out = jnp.where(t >= first + k, jnp.int32(v), out)
    return out


def far_step(q):
    return LFT + q, LFT2 + q, RGT + q, RGT2 + q, 8


def own_step(a, b):
    return a, b, a, b, 0


def describe(t):
    w = jnp.where
    kind = pick(t, 16, ["ABF".index(k) for k, _ in LATE_STEPS])
    late_q = pick(t, 16, [q for _, q in LATE_STEPS])
    is_far = (t >= 16) & (kind == 2)
    q = w(t >= 16, late_q, jnp.maximum(t - 8, 0) // 2)
    second = w(t >= 16, kind, lax.rem(t, 2)) == 1
    a = w(t < 8, 2 * t, w(second, LFT2, LFT) + q)
    b = w(t < 8, 2 * t + 1, w(second, RGT2, RGT) + q)
    return tuple(w(is_far, f, o) for f, o in zip(far_step(q), own_step(a, b)))


def kernel(n, x_hbm, v_hbm, ell_ref, s_ref, out_ref,
           xb, vb, xe, xr, ka, kb, y, pin, cst,
           loc_sem, sx, sv, rx, rv, ps, pr):
    me = lax.axis_index("group")
    core = lax.rem(me, 2)
    sib = me + 1 - 2 * core
    left = lax.rem(me + n - 2, n)
    right = lax.rem(me + 2, n)

    def remote(src, dst, ssem, rsem, dev):
        return pltpu.make_async_remote_copy(
            src_ref=src, dst_ref=dst, send_sem=ssem, recv_sem=rsem,
            device_id={"group": dev}, device_id_type=pl.DeviceIdType.MESH)

    own_x = pltpu.make_async_copy(x_hbm, xb.at[pl.ds(OWN, 8)], loc_sem.at[0])
    own_v = [pltpu.make_async_copy(v_hbm.at[:, pl.ds(i * CH, CH)], vb.at[OWN + i], loc_sem.at[1 + i])
             for i in range(8)]
    own_x.start()
    for c in own_v:
        c.start()
    barrier = pltpu.get_barrier_semaphore()
    for dev in (sib, left, right):
        pl.semaphore_signal(barrier, inc=1, device_id={"group": dev},
                            device_id_type=pl.DeviceIdType.MESH)
    y[...] = jnp.zeros_like(y)
    kb[...] = jnp.zeros_like(kb)
    ell = jnp.full((8, CH), ell_ref[0], jnp.float32)
    cst[0:8, :] = (2.0 * LOG2E) / (2.0 * ell * ell)
    cst[8:16, :] = jnp.log2(jnp.full((8, CH), s_ref[0], jnp.float32))
    own_x.wait()

    def target_ext(slot, tile):
        e, = ext_rows(xb[slot], 3)
        xr[tile] = jnp.concatenate([xb[slot], e], axis=1).T
        return 0

    def own_ext(i, _):
        xe[i], e = ext_rows(xb[i], 0, 3)
        xr[i] = jnp.concatenate([xb[i], e], axis=1).T
        return 0

    lax.fori_loop(0, 8, own_ext, 0)
    for c in own_v:
        c.wait()
    pl.semaphore_wait(barrier, 3)

    def to_left(q, o):
        return (remote(xb.at[OWN + o], xb.at[LFT + q], sx.at[q], rx.at[LFT + q], left),
                remote(vb.at[OWN + o], vb.at[LFT + q], sv.at[q], rv.at[LFT + q], left))

    def to_right(q, o):
        return (remote(xb.at[OWN + o], xb.at[RGT + q], sx.at[8 + q], rx.at[RGT + q], right),
                remote(vb.at[OWN + o], vb.at[RGT + q], sv.at[8 + q], rv.at[RGT + q], right))

    def to_sib():
        return (remote(xb.at[pl.ds(OWN, 8)], xb.at[pl.ds(SIB, 8)], sx.at[16], rx.at[SIB], sib),
                remote(vb.at[pl.ds(OWN, 8)], vb.at[pl.ds(SIB, 8)], sv.at[16], rv.at[SIB], sib))

    def fwd(q):
        return (remote(xb.at[LFT + q], xb.at[LFT2 + q], sx.at[17 + q], rx.at[LFT2 + q], sib),
                remote(vb.at[LFT + q], vb.at[LFT2 + q], sv.at[17 + q], rv.at[LFT2 + q], sib),
                remote(xb.at[RGT + q], xb.at[RGT2 + q], sx.at[25 + q], rx.at[RGT2 + q], sib),
                remote(vb.at[RGT + q], vb.at[RGT2 + q], sv.at[25 + q], rv.at[RGT2 + q], sib))

    def partial_copies(i):
        return (remote(y.at[8 + i], pin.at[i], ps.at[i], pr.at[i], left),
                remote(y.at[12 + i], pin.at[4 + i], ps.at[4 + i], pr.at[4 + i], right))

    for q in range(8):
        for c in to_left(q, (q + 4) % 8) + to_right(q, q):
            c.start()
        if q == 0:
            for c in to_sib():
                c.start()

    def arrive(q):
        for s in (LFT + q, RGT + q):
            remote(xb.at[s], xb.at[s], sx.at[0], rx.at[s], sib).wait_recv()
            remote(vb.at[s], vb.at[s], sv.at[0], rv.at[s], sib).wait_recv()
        for c in fwd(q):
            c.start()

    def arrive2(q):
        for s in (LFT2 + q, RGT2 + q):
            remote(xb.at[s], xb.at[s], sx.at[0], rx.at[s], sib).wait_recv()
            remote(vb.at[s], vb.at[s], sv.at[0], rv.at[s], sib).wait_recv()

    def prep(slots):
        for s in slots:
            xe[s], = ext_rows(xb[s], 0)

    def dot(a, b):
        return jnp.dot(a, b, preferred_element_type=jnp.float32)

    def ext_lhs(slots):
        return jnp.concatenate([jnp.concatenate([xb[s], xe[s]], axis=1) for s in slots], axis=0)

    def k_tile(lhs, tile):
        e = jnp.minimum(dot(lhs, xr[tile]), 0.0) * cst[0:1, :] + cst[8:9, :]
        return jnp.exp2(e).astype(jnp.bfloat16)

    def kv(prev, src, i):
        g = i // 4
        lhs = jnp.concatenate([vb[prev[2 * g]], vb[prev[2 * g + 1]]], axis=1)
        y[prev[4] + i] += dot(lhs, src[i])

    def step(cur, prev, dst, src, halves=2, lag=2):
        for i in range(8):
            g = i // 4
            dst[i, 0:halves * CH, :] = k_tile(ext_lhs(cur[2 * g:2 * g + halves]), cur[4] + i)
            if src is not None and i >= lag:
                kv(prev, src, i - lag)
        if src is not None:
            for i in range(8 - lag, 8):
                kv(prev, src, i)

    def kv_only(prev, src):
        for i in range(8):
            kv(prev, src, i)

    def far_tail(tiles):
        for i in tiles:
            for m, (near, far) in enumerate(((LFT + 7, LFT2 + 7), (RGT + 7, RGT2 + 7))):
                tile = 4 * m + i
                k = k_tile(ext_lhs((far,)), 8 + tile)
                y[8 + tile] += dot(vb[near], ka[tile, 0:CH, :]) + dot(vb[far], k)

    def block(b, _):
        @pl.when(b == 2)
        def _():
            for c in to_sib():
                c.wait_recv()

        qa = pick(b, 3, (0, 1, 0, 2, 3, 3, 4, 5, 5, 6, 6))
        @pl.when((b == 3) | (b == 4) | (b == 6) | (b == 7) | (b == 9) | (b == 10) | (b == 12))
        def _():
            arrive(qa)

        qb = pick(b, 4, (0, 1, 2, 3, 3, 3, 4, 5, 5, 6))
        @pl.when(((b >= 4) & (b <= 7)) | (b == 10) | (b == 11) | (b == 13))
        def _():
            arrive2(qb)

        @pl.when(b == 8)
        def _():
            lax.fori_loop(0, 4, lambda i, _: target_ext(RGT + i, 8 + i), 0)
            lax.fori_loop(0, 4, lambda i, _: target_ext(LFT + i, 12 + i), 0)

        t = 2 * b
        d0, d1, p = describe(t), describe(t + 1), describe(jnp.maximum(t - 1, 0))
        sl = [pick(b, 0, [row[k] for row in PREP]) for k in range(4)]
        prep(sl[0:2])
        step(d0, p, ka, kb)
        prep(sl[2:4])
        step(d1, d0, kb, ka)
        return 0

    lax.fori_loop(0, MAIN_BLOCKS, block, 0)
    last = describe(jnp.int32(2 * MAIN_BLOCKS - 1))
    i32 = jnp.int32
    b6, f7 = own_step(i32(LFT2 + 6), i32(RGT2 + 6)), far_step(i32(7))
    a7, b7 = own_step(i32(LFT + 7), i32(RGT + 7)), own_step(i32(LFT2 + 7), i32(RGT2 + 7))
    arrive(7)
    prep((LFT + 7, RGT + 7))
    step(f7, last, ka, kb, halves=1)
    arrive2(7)
    prep((LFT2 + 7, RGT2 + 7))
    for j in range(2):
        far_tail((2 * j, 2 * j + 1))
        for i in (2 * j, 2 * j + 1):
            for c in partial_copies(i):
                c.start()
    step(b6, None, kb, None)
    step(a7, b6, ka, kb)
    step(b7, a7, kb, ka)
    kv_only(b7, kb)

    for q in range(8):
        for c in to_left(q, (q + 4) % 8) + to_right(q, q) + fwd(q):
            c.wait_send()
    for c in to_sib():
        c.wait_send()
    for i in range(4):
        for c in partial_copies(i):
            c.wait()
        for k in (i, 4 + i):
            out_ref[:, k * CH:(k + 1) * CH] = y[k] + pin[k]


def solution(mesh):
    n = mesh.shape["group"]
    row_spec = P(("tasks", "group"), None)

    def local_fn(x_loc, v_loc, lengthscale, outscale):
        rows, feat = x_loc.shape
        rhs = v_loc.shape[1]
        nc = rows // CH
        bf = jnp.bfloat16
        dma = pltpu.SemaphoreType.DMA
        out = pl.pallas_call(
            functools.partial(kernel, n),
            out_shape=pltpu.VMEM((rhs, rows), jnp.float32),
            in_specs=[pl.BlockSpec(memory_space=pl.ANY), pl.BlockSpec(memory_space=pl.ANY),
                      pl.BlockSpec(memory_space=pltpu.SMEM), pl.BlockSpec(memory_space=pltpu.SMEM)],
            out_specs=pl.BlockSpec(memory_space=pltpu.VMEM),
            scratch_shapes=[
                pltpu.VMEM((6 * nc, CH, feat), bf),
                pltpu.VMEM((6 * nc, rhs, CH), bf),
                pltpu.VMEM((6 * nc, CH, 128), bf),
                pltpu.VMEM((2 * nc, feat + 128, CH), bf),
                pltpu.VMEM((nc, 2 * CH, CH), bf),
                pltpu.VMEM((nc, 2 * CH, CH), bf),
                pltpu.VMEM((2 * nc, rhs, CH), jnp.float32),
                pltpu.VMEM((nc, rhs, CH), jnp.float32),
                pltpu.VMEM((16, CH), jnp.float32),
                dma((9,)), dma((40,)), dma((40,)), dma((6 * nc,)), dma((6 * nc,)), dma((8,)), dma((8,)),
            ],
            compiler_params=pltpu.CompilerParams(
                collective_id=0, has_side_effects=True, vmem_limit_bytes=56 * 2**20),
        )(x_loc.reshape(nc, CH, feat), v_loc.T, lengthscale, outscale)
        return out.T

    return jax.shard_map(local_fn, mesh=mesh, in_specs=(row_spec, row_spec, P(None), P(None)),
                         out_specs=row_spec, check_vma=False)
```

time: 76 us -> 72.8 us (0.958)
  local copies, waits for them, and re-layouts: 3.54 us -> 0.8 us
    reshape x1 -> x0, local copies, waits for them, and re-layouts: 1.67 us -> none  [local_fn(): vt = v_loc.reshape(nc, CH, rhs).transpose(0, 2, 1)]
    unnamed x1, local copies, waits for them, and re-layouts: 1.87 us -> 0.8 us
where the time goes in v2:
time: 72.8 us; the launch traced here: 72.5 us
  Pallas kernels  70.4 us (97%)
  between operations  1.3 us (2%)
  local copies, waits for them, and re-layouts  0.8 us (1%)
    pallas_call x1, Pallas kernels, local_fn(): pl.pallas_call(functools.partial(kernel, n), out_shape=pltpu.VMEM((rhs, r...  70.4 us

profile of v2, /device:TPU:112, one launch (start us, length us, event | category | flops | bytes accessed | tf_op | source)
XLA Modules:
  0.0 72.5 jit_solution(14633268709304301851)
XLA Ops:
  1.3 70.4 %shard_map.46 = f32[64,2048]{1,0:T(8,128)S(1)} custom-call(bf16[8,256,384]{2,1,0:T(8,128)(2,1)} %bitcast.4, bf16[64,2048]{1,0:T(8,128)(2,1)} %bitcast.5, f32[1]{0:T(128)S(6)} %copy.7.ell_ref, f32[1]{0:T(128)S(6)} %copy.8.s_ref), custom_call_target="tpu_custom_call" | custom-call | tf_op jit(solution)/shard_map/pallas_call | solution.py:273
  71.7 0.8 %copy.6 = f32[2048,64]{0,1:T(8,128)} copy(f32[2048,64]{0,1:T(8,128)S(1)} %bitcast.3) | data formatting | bytes 1048576

commit v3 on v2

v3 whole, which is shorter than its diff:
```python
import functools

import jax
import jax.numpy as jnp
from jax import lax
from jax.experimental import pallas as pl
from jax.experimental.pallas import tpu as pltpu
from jax.sharding import PartitionSpec as P

CH = 256
LOG2E = 1.4426950408889634
OWN, SIB, LFT, RGT, LFT2, RGT2 = 0, 8, 16, 24, 32, 40
BLOCKS = 16
LATE_STEPS = (("F", 0), ("F", 1), ("F", 2), ("F", 3), ("F", 4), ("F", 5), ("A", 4), ("B", 4),
              ("F", 6), ("A", 5), ("F", 7), ("B", 5), ("A", 6), ("B", 6), ("A", 7), ("B", 7))
ARRIVE = {3: 0, 4: 1, 5: 2, 7: 3, 8: 4, 9: 5, 11: 6, 12: 7}
ARRIVE2 = {4: 0, 5: 1, 6: 2, 7: 3, 9: 4, 10: 5, 12: 6, 13: 7}
SEND_BLOCK = 14


def half_norms(x):
    xf = x.astype(jnp.float32)
    h = -0.5 * jnp.sum(xf * xf, axis=1, keepdims=True)
    return jnp.broadcast_to(h, (x.shape[0], 128)).T[0:1, :]


def ext_rows(h, first):
    hi = h.astype(jnp.bfloat16).astype(jnp.float32)
    r = jnp.where(h == hi, 0.0, h - hi)
    mid = r.astype(jnp.bfloat16).astype(jnp.float32)
    lo = r - mid
    row = lax.broadcasted_iota(jnp.int32, (8, h.shape[1]), 0)
    e = jnp.where(row < 6, 1.0, 0.0)
    for k, v in enumerate((hi, mid, lo)):
        e = jnp.where(row == first + k, v, e)
    return jnp.concatenate([e, jnp.zeros((120, h.shape[1]), jnp.float32)], axis=0)


PREP = [(0, 1, 2, 3), (4, 5, 6, 7), (8, 9, 10, 11), (12, 13, 14, 15)]
PREP += [(LFT + q, RGT + q, LFT2 + q, RGT2 + q) for q in range(4)]
PREP += [(0, 1, LFT + 4, RGT + 4), (LFT2 + 4, RGT2 + 4, LFT + 5, RGT + 5), (LFT2 + 5, RGT2 + 5, 0, 1),
         (LFT + 6, RGT + 6, 0, 1), (LFT2 + 6, RGT2 + 6, LFT + 7, RGT + 7), (LFT2 + 7, RGT2 + 7, 0, 1),
         (0, 1, 0, 1), (0, 1, 0, 1)]


def pick(t, first, values):
    out = jnp.int32(values[0])
    for k, v in enumerate(values[1:], 1):
        if v != values[k - 1]:
            out = jnp.where(t >= first + k, jnp.int32(v), out)
    return out


def among(b, keys):
    hit = b == keys[0]
    for k in keys[1:]:
        hit = hit | (b == k)
    return hit


def at_block(b, table):
    out, prev = [], min(table.values())
    for k in range(BLOCKS):
        prev = table.get(k, prev)
        out.append(prev)
    return pick(b, 0, out)


def far_step(q):
    return LFT + q, LFT2 + q, RGT + q, RGT2 + q, 8


def own_step(a, b):
    return a, b, a, b, 0


def describe(t):
    w = jnp.where
    kind = pick(t, 16, ["ABF".index(k) for k, _ in LATE_STEPS])
    late_q = pick(t, 16, [q for _, q in LATE_STEPS])
    is_far = (t >= 16) & (kind == 2)
    q = w(t >= 16, late_q, jnp.maximum(t - 8, 0) // 2)
    second = w(t >= 16, kind, lax.rem(t, 2)) == 1
    a = w(t < 8, 2 * t, w(second, LFT2, LFT) + q)
    b = w(t < 8, 2 * t + 1, w(second, RGT2, RGT) + q)
    return tuple(w(is_far, f, o) for f, o in zip(far_step(q), own_step(a, b)))


def kernel(n, x_hbm, v_hbm, ell_ref, s_ref, out_ref,
           xb, vb, hb, xe, xr, ka, kb, y, pin, cst,
           loc_sem, sx, sv, sh, rx, rv, rh, ps, pr):
    me = lax.axis_index("group")
    core = lax.rem(me, 2)
    sib = me + 1 - 2 * core
    left = lax.rem(me + n - 2, n)
    right = lax.rem(me + 2, n)

    def remote(src, dst, ssem, rsem, dev):
        return pltpu.make_async_remote_copy(
            src_ref=src, dst_ref=dst, send_sem=ssem, recv_sem=rsem,
            device_id={"group": dev}, device_id_type=pl.DeviceIdType.MESH)

    own_x = pltpu.make_async_copy(x_hbm, xb.at[pl.ds(OWN, 8)], loc_sem.at[0])
    own_v = [pltpu.make_async_copy(v_hbm.at[:, pl.ds(i * CH, CH)], vb.at[OWN + i], loc_sem.at[1 + i])
             for i in range(8)]
    own_x.start()
    for c in own_v:
        c.start()
    barrier = pltpu.get_barrier_semaphore()
    for dev in (sib, left, right):
        pl.semaphore_signal(barrier, inc=1, device_id={"group": dev},
                            device_id_type=pl.DeviceIdType.MESH)
    y[...] = jnp.zeros_like(y)
    kb[...] = jnp.zeros_like(kb)
    ell = jnp.full((8, CH), ell_ref[0], jnp.float32)
    cst[0:8, :] = (2.0 * LOG2E) / (2.0 * ell * ell)
    cst[8:16, :] = jnp.log2(jnp.full((8, CH), s_ref[0], jnp.float32))
    own_x.wait()

    def target(slot, tile):
        xr[tile, 0:384, :] = xb[slot].T
        xr[tile, 384:512, :] = ext_rows(hb[slot], 3).astype(jnp.bfloat16)
        return 0

    def prep(slots):
        for s in slots:
            xe[s] = ext_rows(hb[s], 0).T.astype(jnp.bfloat16)

    def own_ext(i, _):
        hb[i] = half_norms(xb[i])
        return 0

    lax.fori_loop(0, 8, own_ext, 0)
    for c in own_v:
        c.wait()
    pl.semaphore_wait(barrier, 3)

    def rows_copy(src, dst, k, dev, count=None):
        s, d = (src, dst) if count is None else (pl.ds(src, count), pl.ds(dst, count))
        return tuple(remote(buf.at[s], buf.at[d], ss.at[k], rs.at[dst - SIB], dev)
                     for buf, ss, rs in ((hb, sh, rh), (xb, sx, rx), (vb, sv, rv)))

    def to_left(q, o):
        return rows_copy(OWN + o, LFT + q, 0, left)

    def to_right(q, o):
        return rows_copy(OWN + o, RGT + q, 1, right)

    def to_sib():
        return rows_copy(OWN, SIB, 2, sib, 8)

    def fwd(q):
        return rows_copy(LFT + q, LFT2 + q, 3, sib) + rows_copy(RGT + q, RGT2 + q, 4, sib)

    def all_sent():
        for k, (s, d, dev) in enumerate(((OWN, LFT, left), (OWN, RGT, right), (OWN, SIB, sib),
                                         (LFT, LFT2, sib), (RGT, RGT2, sib))):
            for c in rows_copy(s, d, k, dev, 8):
                c.wait_send()

    def partial_copies():
        return (remote(y.at[pl.ds(8, 4)], pin.at[pl.ds(0, 4)], ps.at[0], pr.at[0], left),
                remote(y.at[pl.ds(12, 4)], pin.at[pl.ds(4, 4)], ps.at[1], pr.at[1], right))

    for q in range(8):
        for c in to_left(q, (q + 4) % 8) + to_right(q, q):
            c.start()
        if q == 0:
            for c in to_sib():
                c.start()

    def received(slot):
        for c in rows_copy(slot, slot, 0, sib):
            c.wait_recv()

    def arrive(q):
        received(LFT + q)
        received(RGT + q)
        for c in fwd(q):
            c.start()

    def arrive2(q):
        received(LFT2 + q)
        received(RGT2 + q)

    lax.fori_loop(0, 8, lambda i, _: target(OWN + i, i), 0)

    def dot(a, b):
        return jnp.dot(a, b, preferred_element_type=jnp.float32)

    def ext_lhs(slots):
        return jnp.concatenate([jnp.concatenate([xb[s], xe[s]], axis=1) for s in slots], axis=0)

    def k_tile(lhs, tile):
        e = jnp.minimum(dot(lhs, xr[tile]), 0.0) * cst[0:1, :] + cst[8:9, :]
        return jnp.exp2(e).astype(jnp.bfloat16)

    def kv(prev, src, i):
        g = i // 4
        lhs = jnp.concatenate([vb[prev[2 * g]], vb[prev[2 * g + 1]]], axis=1)
        y[prev[4] + i] += dot(lhs, src[i])

    def step(cur, prev, dst, src, halves=2, lag=2):
        for i in range(8):
            g = i // 4
            dst[i, 0:halves * CH, :] = k_tile(ext_lhs(cur[2 * g:2 * g + halves]), cur[4] + i)
            if src is not None and i >= lag:
                kv(prev, src, i - lag)
        if src is not None:
            for i in range(8 - lag, 8):
                kv(prev, src, i)

    def block(b, _):
        @pl.when(b == 2)
        def _():
            for c in to_sib():
                c.wait_recv()

        @pl.when(among(b, tuple(ARRIVE)))
        def _():
            arrive(at_block(b, ARRIVE))

        @pl.when(among(b, tuple(ARRIVE2)))
        def _():
            arrive2(at_block(b, ARRIVE2))

        @pl.when(b == SEND_BLOCK)
        def _():
            for c in partial_copies():
                c.start()

        @pl.when(b == 8)
        def _():
            lax.fori_loop(0, 4, lambda i, _: target(RGT + i, 8 + i), 0)
            lax.fori_loop(0, 4, lambda i, _: target(LFT + i, 12 + i), 0)

        t = 2 * b
        d0, d1, p = describe(t), describe(t + 1), describe(jnp.maximum(t - 1, 0))
        sl = [pick(b, 0, [row[k] for row in PREP]) for k in range(4)]
        prep(sl[0:2])
        step(d0, p, ka, kb)
        prep(sl[2:4])
        step(d1, d0, kb, ka)
        return 0

    lax.fori_loop(0, BLOCKS, block, 0)
    i32 = jnp.int32
    last = own_step(i32(LFT2 + 7), i32(RGT2 + 7))
    for i in range(8):
        kv(last, kb, i)
    all_sent()
    for c in partial_copies():
        c.wait()
    for i in range(8):
        out_ref[:, i * CH:(i + 1) * CH] = y[i] + pin[i]


def solution(mesh):
    n = mesh.shape["group"]
    row_spec = P(("tasks", "group"), None)

    def local_fn(x_loc, v_loc, lengthscale, outscale):
        rows, feat = x_loc.shape
        rhs = v_loc.shape[1]
        nc = rows // CH
        bf = jnp.bfloat16
        dma = pltpu.SemaphoreType.DMA
        out = pl.pallas_call(
            functools.partial(kernel, n),
            out_shape=pltpu.VMEM((rhs, rows), jnp.float32),
            in_specs=[pl.BlockSpec(memory_space=pl.ANY), pl.BlockSpec(memory_space=pl.ANY),
                      pl.BlockSpec(memory_space=pltpu.SMEM), pl.BlockSpec(memory_space=pltpu.SMEM)],
            out_specs=pl.BlockSpec(memory_space=pltpu.VMEM),
            scratch_shapes=[
                pltpu.VMEM((6 * nc, CH, feat), bf),
                pltpu.VMEM((6 * nc, rhs, CH), bf),
                pltpu.VMEM((6 * nc, 1, CH), jnp.float32),
                pltpu.VMEM((6 * nc, CH, 128), bf),
                pltpu.VMEM((2 * nc, feat + 128, CH), bf),
                pltpu.VMEM((nc, 2 * CH, CH), bf),
                pltpu.VMEM((nc, 2 * CH, CH), bf),
                pltpu.VMEM((2 * nc, rhs, CH), jnp.float32),
                pltpu.VMEM((nc, rhs, CH), jnp.float32),
                pltpu.VMEM((16, CH), jnp.float32),
                dma((9,)), dma((5,)), dma((5,)), dma((5,)), dma((5 * nc,)), dma((5 * nc,)), dma((5 * nc,)),
                dma((2,)), dma((2,)),
            ],
            compiler_params=pltpu.CompilerParams(
                collective_id=0, has_side_effects=True, vmem_limit_bytes=56 * 2**20),
        )(x_loc.reshape(nc, CH, feat), v_loc.T, lengthscale, outscale)
        return out.T

    return jax.shard_map(local_fn, mesh=mesh, in_specs=(row_spec, row_spec, P(None), P(None)),
                         out_specs=row_spec, check_vma=False)
```

time: 72.8 us -> 66.4 us (0.912)
  Pallas kernels: 70.4 us -> 63.9 us
    pallas_call x1, Pallas kernels: 70.4 us -> 63.9 us  [local_fn(): pl.pallas_call(functools.partial(kernel, n), out_shape=pltpu.VMEM((rhs, r...]
where the time goes in v3:
time: 66.4 us; the launch traced here: 66 us
  Pallas kernels  63.9 us (96%)
  between operations  1.3 us (2%)
  local copies, waits for them, and re-layouts  0.8 us (1%)
    pallas_call x1, Pallas kernels, local_fn(): pl.pallas_call(functools.partial(kernel, n), out_shape=pltpu.VMEM((rhs, r...  63.9 us

profile of v3, /device:TPU:112, one launch (start us, length us, event | category | flops | bytes accessed | tf_op | source)
XLA Modules:
  0.0 66.0 jit_solution(15961776261168057418)
XLA Ops:
  1.3 63.9 %shard_map.46 = f32[64,2048]{1,0:T(8,128)S(1)} custom-call(bf16[8,256,384]{2,1,0:T(8,128)(2,1)} %bitcast.4, bf16[64,2048]{1,0:T(8,128)(2,1)} %bitcast.5, f32[1]{0:T(128)S(6)} %copy.7.ell_ref, f32[1]{0:T(128)S(6)} %copy.8.s_ref), custom_call_target="tpu_custom_call" | custom-call | tf_op jit(solution)/shard_map/pallas_call | solution.py:268
  65.2 0.8 %copy.6 = f32[2048,64]{0,1:T(8,128)} copy(f32[2048,64]{0,1:T(8,128)S(1)} %bitcast.3) | data formatting | bytes 1048576

commit v4 on v3

--- a/solution.py
+++ b/solution.py
@@ -13,8 +13,9 @@
 BLOCKS = 16
 LATE_STEPS = (("F", 0), ("F", 1), ("F", 2), ("F", 3), ("F", 4), ("F", 5), ("A", 4), ("B", 4),
               ("F", 6), ("A", 5), ("F", 7), ("B", 5), ("A", 6), ("B", 6), ("A", 7), ("B", 7))
-ARRIVE = {3: 0, 4: 1, 5: 2, 7: 3, 8: 4, 9: 5, 11: 6, 12: 7}
-ARRIVE2 = {4: 0, 5: 1, 6: 2, 7: 3, 9: 4, 10: 5, 12: 6, 13: 7}
+GROUPS = ((0, 2), (2, 2), (4, 2), (6, 1), (7, 1))
+ARRIVE = {2: {4: 0, 6: 2, 9: 4}, 1: {11: 6, 12: 7}}
+ARRIVE2 = {2: {5: 0, 7: 2, 10: 4}, 1: {12: 6, 13: 7}}
 SEND_BLOCK = 14
 
 
@@ -37,8 +38,8 @@
 
 
 PREP = [(0, 1, 2, 3), (4, 5, 6, 7), (8, 9, 10, 11), (12, 13, 14, 15)]
-PREP += [(LFT + q, RGT + q, LFT2 + q, RGT2 + q) for q in range(4)]
-PREP += [(0, 1, LFT + 4, RGT + 4), (LFT2 + 4, RGT2 + 4, LFT + 5, RGT + 5), (LFT2 + 5, RGT2 + 5, 0, 1),
+PREP += [(a + q, b + q, a + q + 1, b + q + 1) for q in (0, 2) for a, b in ((LFT, RGT), (LFT2, RGT2))]
+PREP += [(0, 1, 0, 1), (LFT + 4, RGT + 4, LFT + 5, RGT + 5), (LFT2 + 4, RGT2 + 4, LFT2 + 5, RGT2 + 5),
          (LFT + 6, RGT + 6, 0, 1), (LFT2 + 6, RGT2 + 6, LFT + 7, RGT + 7), (LFT2 + 7, RGT2 + 7, 0, 1),
          (0, 1, 0, 1), (0, 1, 0, 1)]
 
@@ -79,8 +80,9 @@
     kind = pick(t, 16, ["ABF".index(k) for k, _ in LATE_STEPS])
     late_q = pick(t, 16, [q for _, q in LATE_STEPS])
     is_far = (t >= 16) & (kind == 2)
-    q = w(t >= 16, late_q, jnp.maximum(t - 8, 0) // 2)
-    second = w(t >= 16, kind, lax.rem(t, 2)) == 1
+    u = jnp.maximum(t - 8, 0)
+    q = w(t >= 16, late_q, 2 * (u // 4) + lax.rem(u, 2))
+    second = w(t >= 16, kind, lax.rem(u // 2, 2)) == 1
     a = w(t < 8, 2 * t, w(second, LFT2, LFT) + q)
     b = w(t < 8, 2 * t + 1, w(second, RGT2, RGT) + q)
     return tuple(w(is_far, f, o) for f, o in zip(far_step(q), own_step(a, b)))
@@ -135,22 +137,21 @@
         c.wait()
     pl.semaphore_wait(barrier, 3)
 
-    def rows_copy(src, dst, k, dev, count=None):
-        s, d = (src, dst) if count is None else (pl.ds(src, count), pl.ds(dst, count))
-        return tuple(remote(buf.at[s], buf.at[d], ss.at[k], rs.at[dst - SIB], dev)
+    def rows_copy(src, dst, k, dev, count):
+        return tuple(remote(buf.at[pl.ds(src, count)], buf.at[pl.ds(dst, count)], ss.at[k], rs.at[dst - SIB], dev)
                      for buf, ss, rs in ((hb, sh, rh), (xb, sx, rx), (vb, sv, rv)))
 
-    def to_left(q, o):
-        return rows_copy(OWN + o, LFT + q, 0, left)
-
-    def to_right(q, o):
-        return rows_copy(OWN + o, RGT + q, 1, right)
+    def to_left(q, count):
+        return rows_copy(OWN + (q + 4) % 8, LFT + q, 0, left, count)
+
+    def to_right(q, count):
+        return rows_copy(OWN + q, RGT + q, 1, right, count)
 
     def to_sib():
         return rows_copy(OWN, SIB, 2, sib, 8)
 
-    def fwd(q):
-        return rows_copy(LFT + q, LFT2 + q, 3, sib) + rows_copy(RGT + q, RGT2 + q, 4, sib)
+    def fwd(q, count):
+        return rows_copy(LFT + q, LFT2 + q, 3, sib, count) + rows_copy(RGT + q, RGT2 + q, 4, sib, count)
 
     def all_sent():
         for k, (s, d, dev) in enumerate(((OWN, LFT, left), (OWN, RGT, right), (OWN, SIB, sib),
@@ -162,26 +163,26 @@
         return (remote(y.at[pl.ds(8, 4)], pin.at[pl.ds(0, 4)], ps.at[0], pr.at[0], left),
                 remote(y.at[pl.ds(12, 4)], pin.at[pl.ds(4, 4)], ps.at[1], pr.at[1], right))
 
-    for q in range(8):
-        for c in to_left(q, (q + 4) % 8) + to_right(q, q):
+    for q, count in GROUPS:
+        for c in to_left(q, count) + to_right(q, count):
             c.start()
         if q == 0:
             for c in to_sib():
                 c.start()
 
-    def received(slot):
-        for c in rows_copy(slot, slot, 0, sib):
+    def received(slot, count):
+        for c in rows_copy(slot, slot, 0, sib, count):
             c.wait_recv()
 
-    def arrive(q):
-        received(LFT + q)
-        received(RGT + q)
-        for c in fwd(q):
+    def arrive(q, count):
+        received(LFT + q, count)
+        received(RGT + q, count)
+        for c in fwd(q, count):
             c.start()
 
-    def arrive2(q):
-        received(LFT2 + q)
-        received(RGT2 + q)
+    def arrive2(q, count):
+        received(LFT2 + q, count)
+        received(RGT2 + q, count)
 
     lax.fori_loop(0, 8, lambda i, _: target(OWN + i, i), 0)
 
@@ -192,7 +193,7 @@
         return jnp.concatenate([jnp.concatenate([xb[s], xe[s]], axis=1) for s in slots], axis=0)
 
     def k_tile(lhs, tile):
-        e = jnp.minimum(dot(lhs, xr[tile]), 0.0) * cst[0:1, :] + cst[8:9, :]
+        e = jnp.minimum(dot(lhs, xr[tile]), 0.0) * cst[0:1, 0:1] + cst[8:9, 0:1]
         return jnp.exp2(e).astype(jnp.bfloat16)
 
     def kv(prev, src, i):
@@ -216,13 +217,11 @@
             for c in to_sib():
                 c.wait_recv()
 
-        @pl.when(among(b, tuple(ARRIVE)))
-        def _():
-            arrive(at_block(b, ARRIVE))
-
-        @pl.when(among(b, tuple(ARRIVE2)))
-        def _():
-            arrive2(at_block(b, ARRIVE2))
+        for table, event in ((ARRIVE, arrive), (ARRIVE2, arrive2)):
+            for count, at in table.items():
+                @pl.when(among(b, tuple(at)))
+                def _(event=event, at=at, count=count):
+                    event(at_block(b, at), count)
 
         @pl.when(b == SEND_BLOCK)
         def _():

time: 66.4 us -> 64.3 us (0.968)
  Pallas kernels: 63.9 us -> 62.1 us
    pallas_call x1, Pallas kernels: 63.9 us -> 62.1 us  [local_fn(): pl.pallas_call(functools.partial(kernel, n), out_shape=pltpu.VMEM((rhs, r...]
where the time goes in v4:
time: 64.3 us; the launch traced here: 64.2 us
  Pallas kernels  62.1 us (97%)
  between operations  1.3 us (2%)
  local copies, waits for them, and re-layouts  0.8 us (1%)
    pallas_call x1, Pallas kernels, local_fn(): pl.pallas_call(functools.partial(kernel, n), out_shape=pltpu.VMEM((rhs, r...  62.1 us

profile of v4, /device:TPU:112, one launch (start us, length us, event | category | flops | bytes accessed | tf_op | source)
XLA Modules:
  0.0 64.2 jit_solution(4683654046941715349)
XLA Ops:
  1.3 62.1 %shard_map.46 = f32[64,2048]{1,0:T(8,128)S(1)} custom-call(bf16[8,256,384]{2,1,0:T(8,128)(2,1)} %bitcast.4, bf16[64,2048]{1,0:T(8,128)(2,1)} %bitcast.5, f32[1]{0:T(128)S(6)} %copy.7.ell_ref, f32[1]{0:T(128)S(6)} %copy.8.s_ref), custom_call_target="tpu_custom_call" | custom-call | tf_op jit(solution)/shard_map/pallas_call | solution.py:267
  63.4 0.8 %copy.6 = f32[2048,64]{0,1:T(8,128)} copy(f32[2048,64]{0,1:T(8,128)S(1)} %bitcast.3) | data formatting | bytes 1048576

commit v5 on v4

--- a/solution.py
+++ b/solution.py
@@ -132,7 +132,6 @@
         hb[i] = half_norms(xb[i])
         return 0
 
-    lax.fori_loop(0, 8, own_ext, 0)
     for c in own_v:
         c.wait()
     pl.semaphore_wait(barrier, 3)
@@ -163,12 +162,17 @@
         return (remote(y.at[pl.ds(8, 4)], pin.at[pl.ds(0, 4)], ps.at[0], pr.at[0], left),
                 remote(y.at[pl.ds(12, 4)], pin.at[pl.ds(4, 4)], ps.at[1], pr.at[1], right))
 
-    for q, count in GROUPS:
+    first, rest = GROUPS[0], GROUPS[1:]
+    early = [to_left(*first), to_right(*first), to_sib()]
+    for c in early[0][1:] + early[1][1:] + early[2][1:]:
+        c.start()
+    lax.fori_loop(0, 8, own_ext, 0)
+    lax.fori_loop(0, 8, lambda i, _: target(OWN + i, i), 0)
+    for copies in early:
+        copies[0].start()
+    for q, count in rest:
         for c in to_left(q, count) + to_right(q, count):
             c.start()
-        if q == 0:
-            for c in to_sib():
-                c.start()
 
     def received(slot, count):
         for c in rows_copy(slot, slot, 0, sib, count):
@@ -183,8 +187,6 @@
     def arrive2(q, count):
         received(LFT2 + q, count)
         received(RGT2 + q, count)
-
-    lax.fori_loop(0, 8, lambda i, _: target(OWN + i, i), 0)
 
     def dot(a, b):
         return jnp.dot(a, b, preferred_element_type=jnp.float32)

time: 64.3 us -> 64 us (level)
  no operation moved by 1% of the time
where the time goes in v5:
time: 64 us; the launch traced here: 63.9 us
  Pallas kernels  61.8 us (97%)
  between operations  1.3 us (2%)
  local copies, waits for them, and re-layouts  0.8 us (1%)
    pallas_call x1, Pallas kernels, local_fn(): pl.pallas_call(functools.partial(kernel, n), out_shape=pltpu.VMEM((rhs, r...  61.8 us

profile of v5, /device:TPU:112, one launch (start us, length us, event | category | flops | bytes accessed | tf_op | source)
XLA Modules:
  0.0 63.9 jit_solution(11504809442227035458)
XLA Ops:
  1.3 61.8 %shard_map.46 = f32[64,2048]{1,0:T(8,128)S(1)} custom-call(bf16[8,256,384]{2,1,0:T(8,128)(2,1)} %bitcast.4, bf16[64,2048]{1,0:T(8,128)(2,1)} %bitcast.5, f32[1]{0:T(128)S(6)} %copy.7.ell_ref, f32[1]{0:T(128)S(6)} %copy.8.s_ref), custom_call_target="tpu_custom_call" | custom-call | tf_op jit(solution)/shard_map/pallas_call | solution.py:269
  63.1 0.8 %copy.6 = f32[2048,64]{0,1:T(8,128)} copy(f32[2048,64]{0,1:T(8,128)S(1)} %bitcast.3) | data formatting | bytes 1048576

commit v6 on v5

--- a/solution.py
+++ b/solution.py
@@ -166,8 +166,8 @@
     early = [to_left(*first), to_right(*first), to_sib()]
     for c in early[0][1:] + early[1][1:] + early[2][1:]:
         c.start()
-    lax.fori_loop(0, 8, own_ext, 0)
-    lax.fori_loop(0, 8, lambda i, _: target(OWN + i, i), 0)
+    lax.fori_loop(0, 2, lambda i, _: [own_ext(4 * i + k, 0) for k in range(4)][0], 0)
+    lax.fori_loop(0, 2, lambda i, _: [target(OWN + 4 * i + k, 4 * i + k) for k in range(4)][0], 0)
     for copies in early:
         copies[0].start()
     for q, count in rest:
@@ -232,8 +232,8 @@
 
         @pl.when(b == 8)
         def _():
-            lax.fori_loop(0, 4, lambda i, _: target(RGT + i, 8 + i), 0)
-            lax.fori_loop(0, 4, lambda i, _: target(LFT + i, 12 + i), 0)
+            lax.fori_loop(0, 2, lambda i, _: [target(base + 2 * i + k, tile + 2 * i + k)
+                                              for base, tile in ((RGT, 8), (LFT, 12)) for k in range(2)][0], 0)
 
         t = 2 * b
         d0, d1, p = describe(t), describe(t + 1), describe(jnp.maximum(t - 1, 0))

time: 64 us -> 63.7 us (level)
  no operation moved by 1% of the time
where the time goes in v6:
time: 63.7 us; the launch traced here: 63.6 us
  Pallas kernels  61.5 us (97%)
  between operations  1.3 us (2%)
  local copies, waits for them, and re-layouts  0.8 us (1%)
    pallas_call x1, Pallas kernels, local_fn(): pl.pallas_call(functools.partial(kernel, n), out_shape=pltpu.VMEM((rhs, r...  61.5 us

profile of v6, /device:TPU:112, one launch (start us, length us, event | category | flops | bytes accessed | tf_op | source)
XLA Modules:
  0.0 63.6 jit_solution(16527611494614331120)
XLA Ops:
  1.3 61.5 %shard_map.46 = f32[64,2048]{1,0:T(8,128)S(1)} custom-call(bf16[8,256,384]{2,1,0:T(8,128)(2,1)} %bitcast.4, bf16[64,2048]{1,0:T(8,128)(2,1)} %bitcast.5, f32[1]{0:T(128)S(6)} %copy.7.ell_ref, f32[1]{0:T(128)S(6)} %copy.8.s_ref), custom_call_target="tpu_custom_call" | custom-call | tf_op jit(solution)/shard_map/pallas_call | solution.py:269
  62.8 0.8 %copy.6 = f32[2048,64]{0,1:T(8,128)} copy(f32[2048,64]{0,1:T(8,128)S(1)} %bitcast.3) | data formatting | bytes 1048576
